TPU v7x, 32 devices: a whole 2x2x4 slice. The times are simulated.
32 devices in a mesh: slab: 8 (over z, x), cross: 4 (over y, core).
Axes of the slice: x: 2, y: 2, z: 4, core: 2. Of those that a mesh axis runs over, the one named last changes fastest.
Arguments:
- gas_state: float32 [16, 64, 8192], P(None, 'slab', 'cross'), may hold values from -4 to 4, as said below
- parcel_record: float32 [5, 131072], P(None, ('slab', 'cross')), may hold values from -4 to 4, as said below
- condensed_shares: float32 [12, 131072], P(None, ('slab', 'cross')), may hold values from 0.02 to 0.2
- surface_steam_factor: float32 [12], replicated, may hold values from 0.2 to 2
- fine_cell: int32 [131072], P(('slab', 'cross')), may hold values from 0 to 20479, as said below
- block_counts: int32 [1024], P(('slab', 'cross')), may hold values from 16 to 128, as said below
Outputs:
- parcel_next: float32 [5, 131072], P(None, ('slab', 'cross'))
- fine_source: float32 [16, 64, 8192], P(None, 'slab', 'cross')
- correction: float32 [64, 4096], replicated
Inputs may be any that keep to these rules, and one draw needn't show every extreme that they name: fine_cell is plane * 2048 + k, with plane 0 and 9 the neighbouring slabs' last and first planes; it never points outside the gas mesh, and is non-decreasing over each device's 4096 slots. The live parcels of each aligned block of 128 slots are its first block_counts slots; the last block of each device's 4096 slots is full. `gas_state`: rows 0 to 2 velocity, row 3 temperature from 1 to 2, rows 4 on vapour fractions from 0 to 0.1. `parcel_record`: rows 0 to 2 velocity, row 3 temperature from 0.6 to 0.9, row 4 mass from 0.5 to 3.
All inputs are finite; a program needn't handle non-finite values.
Results may differ from a plain program's by a relative error of at most 0.00002.
Values sent between devices are 32-bit elements; how exact they have to be, the bound alone decides.
No kernel may reach another device: no remote copies, remote signals or barrier semaphores. Data moves between devices by JAX's collectives and lax.ppermute only.
A program may use at most 64 MiB of HBM per device.

v0:
```python
import jax
import jax.numpy as jnp
from jax import lax
from jax.sharding import PartitionSpec as P

BLOCK = 128
COARSE = 64
SWEEPS = 4
drag_rate = 0.5
evap_rate = 0.08
warming_speed = 0.3
latent_boiling_energy = 0.5
vapour_heat = 1.5
volume_inverse = 4.0


def with_halo(shard, sides, width):
    for axis, dim in sides:
        devices, length = (lax.axis_size(axis), shard.shape[dim])
        up = [(i, (i + 1) % devices) for i in range(devices - 1)]
        down = [(j, i) for i, j in up]
        last = lax.slice_in_dim(shard, length - width, length, axis=dim)
        leading = lax.slice_in_dim(shard, 0, width, axis=dim)
        before = lax.ppermute(last, axis, up)
        after = lax.ppermute(leading, axis, down)
        shard = jnp.concatenate([before, shard, after], axis=dim)
    return shard


def shifted(shard, axis, by):
    devices = lax.axis_size(axis)
    pairs = [(i, i + by) for i in range(devices) if 0 <= i + by < devices]
    return lax.ppermute(shard, axis, pairs)


def partner(shard, axis, bit):
    return lax.ppermute(shard, axis, [(i, i ^ 1 << bit) for i in range(lax.axis_size(axis))])


def advance(
    ambient_layer_fields, parcel_record, condensed_shares, surface_steam_factor, alive_mask
):
    gas_velocity = ambient_layer_fields[0:3]
    ambient_thermal_level = ambient_layer_fields[3]
    gas_vapour = ambient_layer_fields[4:]
    parcel_velocity = parcel_record[0:3]
    parcel_thermal_level = parcel_record[3]
    parcel_weight_amount = parcel_record[4]
    slip_velocity = gas_velocity - parcel_velocity
    slip_squared = jnp.sum(slip_velocity * slip_velocity, axis=0)
    drag_factor = (
        drag_rate
        * jnp.power(parcel_weight_amount, -2.0 / 3.0)
        * (1.0 + 0.15 * jnp.power(slip_squared + 1.0, 0.3435))
    )
    following_motion = (parcel_velocity + drag_factor * gas_velocity) / (1.0 + drag_factor)
    surface_steam_share = (
        condensed_shares
        * surface_steam_factor[:, None]
        * jnp.exp(2.0 * (parcel_thermal_level - 0.75))
    )
    species_rates = evap_rate * parcel_weight_amount * (surface_steam_share - gas_vapour)
    evaporated_weight = jnp.sum(species_rates, axis=0)
    thermal_exchange = (
        warming_speed
        * (ambient_thermal_level - parcel_thermal_level)
        * jnp.power(parcel_weight_amount, 1.0 / 3.0)
    )
    following_thermal_level = (
        parcel_thermal_level
        + (thermal_exchange - latent_boiling_energy * evaporated_weight) / parcel_weight_amount
    )
    following_weight = parcel_weight_amount - evaporated_weight
    momentum_terms = (
        parcel_weight_amount * (parcel_velocity - following_motion)
        + evaporated_weight * following_motion
    )
    energy_terms = vapour_heat * evaporated_weight - thermal_exchange
    source_terms = jnp.concatenate([momentum_terms, energy_terms[None], species_rates], axis=0)
    source_terms = source_terms * (alive_mask * volume_inverse)
    updated_parcel_record = jnp.concatenate(
        [following_motion, following_thermal_level[None], following_weight[None]], axis=0
    )
    parcel_next = jnp.where(alive_mask[None] > 0.5, updated_parcel_record, parcel_record)
    return (source_terms, parcel_next, evaporated_weight * alive_mask)


def neighbours(values_grid):
    edge = values_grid.shape[0]
    padded_x = jnp.pad(values_grid, ((1, 1), (0, 0)))
    summed = padded_x[2:] + padded_x[:-2]
    padded_y = jnp.pad(values_grid, ((0, 0), (edge, edge)))
    summed = summed + padded_y[:, 2 * edge :] + padded_y[:, : -2 * edge]
    padded_z = jnp.pad(values_grid, ((0, 0), (1, 1)))
    depth = jnp.arange(values_grid.shape[1], dtype=jnp.int32) % edge
    upper_mask = (depth < edge - 1).astype(values_grid.dtype)
    lower_mask = (depth > 0).astype(values_grid.dtype)
    return summed + padded_z[:, 2:] * upper_mask + padded_z[:, :-2] * lower_mask


def relax(coarse_source):
    solution = jnp.zeros_like(coarse_source)
    for sweep in range(SWEEPS):
        solution = (neighbours(solution) + coarse_source) / 6.0
    return solution


def body(gas_state, parcel_record, condensed_shares, surface_steam_factor, fine_cell, block_counts):
    fields = gas_state.shape[0]
    planes = gas_state.shape[1]
    cross_cells = gas_state.shape[2]
    slab_count = lax.axis_size("slab")
    cross_count = lax.axis_size("cross")
    slab_index = lax.axis_index("slab")
    padded_gas = with_halo(gas_state, (("slab", 1),), 1)
    gas_flat = padded_gas.reshape(fields, (planes + 2) * cross_cells)
    ambient_layer_fields = jnp.take(gas_flat, fine_cell, axis=1)
    slot_in_block = jnp.arange(BLOCK, dtype=jnp.int32)
    alive_mask = (slot_in_block[None, :] < block_counts[:, None]).reshape(-1).astype(jnp.float32)
    source_terms, parcel_next, evaporated_weight = advance(
        ambient_layer_fields, parcel_record, condensed_shares, surface_steam_factor, alive_mask
    )
    extended = (
        jnp.zeros((fields, (planes + 2) * cross_cells), jnp.float32)
        .at[:, fine_cell]
        .add(source_terms)
    )
    extended = extended.reshape(fields, planes + 2, cross_cells)
    from_above = shifted(extended[:, 0], "slab", -1)
    from_below = shifted(extended[:, planes + 1], "slab", 1)
    fine_source = extended[:, 1 : planes + 1]
    fine_source = fine_source.at[:, planes - 1].add(from_above)
    fine_source = fine_source.at[:, 0].add(from_below)
    squared = COARSE * COARSE
    fine_per_coarse = planes * slab_count // COARSE
    cross_per_coarse = cross_cells * cross_count // squared
    column_count = cross_cells // cross_per_coarse
    mass_cells = jnp.sum(fine_source[4:], axis=0) * (1.0 / volume_inverse)
    if fine_per_coarse <= planes:
        own_planes = planes // fine_per_coarse
        owned = mass_cells.reshape(own_planes, fine_per_coarse, column_count, cross_per_coarse)
        owned = jnp.sum(owned, axis=(1, 3)).reshape(-1)
    else:
        group = fine_per_coarse // planes
        owned = jnp.sum(mass_cells.reshape(planes, column_count, cross_per_coarse), axis=(0, 2))
        levels = group.bit_length() - 1
        for level in range(levels - 1, -1, -1):
            half = owned.shape[0] // 2
            upper_side = slab_index // 2**level % 2 == 1
            lower_part = owned[:half]
            upper_part = owned[half:]
            keep = jnp.where(upper_side, upper_part, lower_part)
            send = jnp.where(upper_side, lower_part, upper_part)
            owned = keep + partner(send, "slab", level)
    gathered = lax.all_gather(owned[None], ("slab", "cross"), axis=0, tiled=True)
    if fine_per_coarse <= planes:
        gathered = gathered.reshape(
            slab_count, cross_count, planes // fine_per_coarse, column_count
        )
        coarse_source = jnp.transpose(gathered, (0, 2, 1, 3)).reshape(COARSE, squared)
    else:
        group = fine_per_coarse // planes
        gathered = gathered.reshape(COARSE, group, cross_count, column_count // group)
        coarse_source = jnp.transpose(gathered, (0, 2, 1, 3)).reshape(COARSE, squared)
    correction = relax(coarse_source)
    return (parcel_next, fine_source, correction)


def solution(mesh):
    in_specs = (
        P(None, "slab", "cross"),
        P(None, ("slab", "cross")),
        P(None, ("slab", "cross")),
        P(),
        P(("slab", "cross")),
        P(("slab", "cross")),
    )
    out_specs = (P(None, ("slab", "cross")), P(None, "slab", "cross"), P())
    return jax.shard_map(body, mesh=mesh, in_specs=in_specs, out_specs=out_specs, check_vma=False)
```

profile of v0, /device:TPU:0, one launch (start us, length us, event | category | flops | bytes accessed | tf_op | source)
XLA Modules:
  0.0 172.7 jit_solution(5224186087210317424)
XLA Ops:
  7.2 2.0 %fusion.50 = (f32[16,1,2048]{2,1,0:T(1,128)S(1)}, f32[16,1,2048]{2,1,0:T(1,128)S(1)}) fusion(f32[16,8,2048]{2,1,0:T(8,128)} %param.10), kind=kLoop, calls=%fused_computation.91 | loop fusion | bytes 524288 | tf_op jit(solution)/shard_map/slice | solution.py:22
  9.2 4.9 %collective-permute-start = (f32[16,1,2048]{2,0,1:T(8,128)S(1)}, f32[16,1,2048]{2,0,1:T(8,128)S(1)}, u32[]{:S(2)}, u32[]{:S(2)}) collective-permute-start(f32[16,1,2048]{2,0,1:T(8,128)S(1)} %copy.117), channel_id=1, source_target_pairs={{0,4},{4,8},{8,12},{12,16},{16,20},{20,24},{24,28},{1,5},{5,9},{9,... | collective-permute-start | bytes 393224 | tf_op jit(solution)/shard_map/ppermute | solution.py:24
  14.2 1.3 collective-permute-start.1
  15.5 0.7 compare_select_fusion
  16.2 0.7 compare_and_fusion
  16.9 0.7 select_bitcast_fusion.1
  17.7 0.1 copy.105
  17.8 3.2 %collective-permute-done.1 = f32[16,1,2048]{2,0,1:T(8,128)S(1)} collective-permute-done((f32[16,1,2048]{2,0,1:T(8,128)S(1)}, f32[16,1,2048]{2,0,1:T(8,128)S(1)}, u32[]{:S(2)}, u32[]{:S(2)}) %collective-permute-start.1) | collective-permute-done | bytes 131104 | tf_op jit(solution)/shard_map/ppermute | solution.py:25
  21.0 0.1 copy.106
  21.2 0.4 pad_maximum_fusion
  21.6 5.4 %copy.107 = f32[16,10,2048]{0,2,1:T(8,128)} copy(f32[16,10,2048]{2,1,0:T(8,128)S(1)} %pad_maximum_fusion) | data formatting | bytes 2621440 | tf_op jit(solution)/shard_map/concatenate | solution.py:26
  27.0 14.8 %gather_fusion = f32[4096,16]{1,0:T(8,128)S(1)} fusion(f32[16,20480]{0,1:T(8,128)} %bitcast.39, s32[4096]{0:T(1024)S(1)} %get-tuple-element.61), kind=kCustom, calls=%fused_computation | custom fusion | bytes 540672 | tf_op jit(solution)/shard_map/jit(_take)/gather | solution.py:117
  41.8 0.6 copy.108
  42.4 0.1 multiply_reduce_fusion
  42.5 0.2 broadcast_add_fusion
  42.7 0.1 fusion.47
  42.9 0.2 multiply_subtract_fusion
  43.1 0.1 multiply_add_fusion
  43.1 0.1 fusion.33
  43.2 0.6 copy.109
  43.8 26.9 %scatter_custom_fusion = f32[16,20480]{0,1:T(8,128)} fusion(s32[4096]{0:T(1024)S(1)} %get-tuple-element.60, f32[4096,16]{1,0:T(8,128)S(1)} %copy.109, f32[]{:T(128)} %constant.122.clone.1), kind=kCustom, calls=%fused_computation.2 | custom fusion | flops 65536 | bytes 1310724 | tf_op jit(solution)/shard_map/scatter-add | solution.py:126
  70.8 2.1 %fusion.49 = (f32[16,1,2048]{0,2,1:T(8,128)S(1)}, f32[16,1,2048]{0,2,1:T(8,128)S(1)}, f32[16,1,2048]{0,2,1:T(8,128)S(1)}) fusion(f32[16,10,2048]{0,2,1:T(8,128)} %bitcast.33), kind=kLoop, calls=%fused_computation.90 | loop fusion | bytes 786432 | tf_op jit(solution)/shard_map/slice | solution.py:130
  72.8 1.0 copy.121
  73.8 1.3 collective-permute-start.2
  75.1 7.3 %slice.196 = f32[16,8,2048]{0,2,1:T(8,128)} slice(f32[16,10,2048]{0,2,1:T(8,128)} %bitcast.34), slice={[0:16], [1:9], [0:2048]} | slice | bytes 2097152 | tf_op jit(solution)/shard_map/slice | solution.py:131
  82.4 5.1 %copy.119 = f32[16,8,2048]{2,0,1:T(8,128)S(1)} copy(f32[16,8,2048]{0,2,1:T(8,128)} %slice.196) | data formatting | bytes 2097152
  87.5 0.3 copy.120
  87.8 0.3 copy.122
  88.1 5.2 %collective-permute-start.3 = (f32[16,2048]{1,0:T(8,128)S(1)}, f32[16,2048]{1,0:T(8,128)S(1)}, u32[]{:S(2)}, u32[]{:S(2)}) collective-permute-start(f32[16,2048]{1,0:T(8,128)S(1)} %bitcast.44), channel_id=1, source_target_pairs={{0,4},{4,8},{8,12},{12,16},{16,20},{20,24},{24,28},{1,5},{5,9},{9,... | collective-permute-start | bytes 393224 | tf_op jit(solution)/shard_map/ppermute | solution.py:33
  93.3 0.9 fusion.35
  94.2 1.4 collective-permute-done.3
  95.6 0.2 slice_reduce_fusion
  95.9 0.3 copy.114
  96.2 1.3 reduce_sum.42
  97.5 0.2 copy.115
  97.7 0.7 reshape.210
  98.4 0.1 fusion.42
  98.5 0.1 divide_add_fusion
  98.5 0.7 maximum_select_fusion
  99.3 1.6 copy.116
  100.8 54.9 %all-gather.3.cloned.1.call-done = f32[32,1,8192]{2,1,0:T(1,128)} async-done(((f32[1,1,8192]{2,1,0:T(1,128)}), f32[32,1,8192]{2,1,0:T(1,128)}) %all-gather.3.cloned.1.call-update) | async-done | bytes 1048592 | tf_op jit(solution)/shard_map/all_gather | solution.py:155
  155.8 3.8 %reduce.5 = f32[32,8192]{1,0:T(8,128)S(1)} reduce(f32[32,1,8192]{2,1,0:T(1,128)} %all-gather.3.cloned.1.call-done, f32[]{:T(128)} %constant.162), dimensions={1}, to_apply=%all-gather.reduce_sub_computation | reduce | bytes 2097156 | tf_op jit(solution)/shard_map/all_gather | solution.py:155
  159.6 0.6 copy.123
  160.2 0.1 broadcast_in_dim.29
  160.3 1.1 fusion.28
  161.4 1.1 fusion.8
  162.6 1.1 fusion.15
  163.7 2.1 %fusion.22 = f32[64,4096]{1,0:T(8,128)} fusion(f32[64,4096]{1,0:T(8,128)S(1)} %bitcast.38, f32[64,4096]{1,0:T(8,128)S(1)} %fusion.15, f32[4096]{0:T(1024)S(1)} %get-tuple-element.63, f32[4096]{0:T(1024)S(1)} %get-tuple-element.62), kind=kLoop, calls=%fused_computation.37 | loop fusion | flops 2359296 | bytes 3178496 | tf_op jit(solution)/shard_map/div | solution.py:104
  (21 shorter events, 0.3 us)
Async XLA Ops:
  7.2 14.0 %copy-start = (f32[16,8,2048]{2,1,0:T(8,128)S(1)}, f32[16,8,2048]{2,1,0:T(8,128)}, u32[]{:S(2)}) copy-start(f32[16,8,2048]{2,1,0:T(8,128)} %param.10) | copy-start | bytes 3145732
  7.2 148.6 %all-gather.3.cloned.1.call-start = ((), (), s32[]{:S(2)}) async-start(), calls=%async_computation | async-start | bytes 1081344 | tf_op jit(solution)/shard_map/all_gather | solution.py:155
  9.2 8.4 %collective-permute-start = (f32[16,1,2048]{2,0,1:T(8,128)S(1)}, f32[16,1,2048]{2,0,1:T(8,128)S(1)}, u32[]{:S(2)}, u32[]{:S(2)}) collective-permute-start(f32[16,1,2048]{2,0,1:T(8,128)S(1)} %copy.117), channel_id=1, source_target_pairs={{0,4},{4,8},{8,12},{12,16},{16,20},{20,24},{24,28},{1,5},{5,9},{9,... | collective-permute-start | bytes 393224 | tf_op jit(solution)/shard_map/ppermute | solution.py:24
  14.2 6.9 %collective-permute-start.1 = (f32[16,1,2048]{2,0,1:T(8,128)S(1)}, f32[16,1,2048]{2,0,1:T(8,128)S(1)}, u32[]{:S(2)}, u32[]{:S(2)}) collective-permute-start(f32[16,1,2048]{2,0,1:T(8,128)S(1)} %copy.118), channel_id=1, source_target_pairs={{4,0},{8,4},{12,8},{16,12},{20,16},{24,20},{28,24},{5,1},{9,5},{13... | collective-permute-start | bytes 393224 | tf_op jit(solution)/shard_map/ppermute | solution.py:25
  27.0 15.4 %copy-start.1 = (f32[5,4096]{1,0:T(8,128)S(1)}, f32[5,4096]{1,0:T(8,128)}, u32[]{:S(2)}) copy-start(f32[5,4096]{1,0:T(8,128)} %param.11) | copy-start | bytes 245764
  41.8 1.0 copy-start.2
  41.8 0.9 copy-start.4
  73.8 19.5 %collective-permute-start.2 = (f32[16,2048]{1,0:T(8,128)}, f32[16,2048]{1,0:T(8,128)}, u32[]{:S(2)}, u32[]{:S(2)}) collective-permute-start(f32[16,2048]{1,0:T(8,128)} %bitcast.13), channel_id=1, source_target_pairs={{4,0},{8,4},{12,8},{16,12},{20,16},{24,20},{28,24},{5,1},{9,5},{13... | collective-permute-start | bytes 393224 | tf_op jit(solution)/shard_map/ppermute | solution.py:33
  88.1 7.5 %collective-permute-start.3 = (f32[16,2048]{1,0:T(8,128)S(1)}, f32[16,2048]{1,0:T(8,128)S(1)}, u32[]{:S(2)}, u32[]{:S(2)}) collective-permute-start(f32[16,2048]{1,0:T(8,128)S(1)} %bitcast.44), channel_id=1, source_target_pairs={{0,4},{4,8},{8,12},{12,16},{16,20},{20,24},{24,28},{1,5},{5,9},{9,... | collective-permute-start | bytes 393224 | tf_op jit(solution)/shard_map/ppermute | solution.py:33
  95.6 2.8 %copy-start.3 = (s32[32]{0:T(128)S(1)}, s32[32]{0:T(128)}, u32[]{:S(2)}) copy-start(s32[32]{0:T(128)} %param.15) | copy-start | bytes 388
Sparse Core Ops, SparseCore 0:
  98.5 57.2 all-gather.2
where the time goes:
time: 173 us
  waiting for transfers between devices  59.6 us (34%)
  local copies, waits for them, and re-layouts  43.2 us (25%)
  other arithmetic  43 us (25%)
  between operations  14.3 us (8%)
  starting transfers between devices  12.7 us (7%)
    all_gather x1, waiting for transfers between devices, body(): lax.all_gather(owned[None], ('slab', 'cross'), axis=0, tiled=True)  54.9 us
    scatter-add x1, other arithmetic, body(): extended = jnp.zeros((fields, (planes + 2) * cross_cells), jnp.float32).a...  26.9 us
    gather x2, local copies, waits for them, and re-layouts, body(): ambient_layer_fields = jnp.take(gas_flat, fine_cell, axis=1)  15.3 us
    unnamed x19, local copies, waits for them, and re-layouts  9.69 us
    slice x1, local copies, waits for them, and re-layouts, body(): fine_source = extended[:, 1:planes + 1]  7.3 us
    ppermute x2, starting transfers between devices, shifted(): return lax.ppermute(shard, axis, pairs)  6.45 us
    div x4, other arithmetic, relax(): solution = (neighbours(solution) + coarse_source) / 6.0  5.57 us
    concatenate x1, local copies, waits for them, and re-layouts, with_halo(): shard = jnp.concatenate([before, shard, after], axis=dim)  5.39 us
  transfers between devices with their start and end apart: 5, of which 3 were waited for; matrix products, arithmetic and copies ran while one was open for 11% of the time, Pallas kernels for 0%

commit v1 on v0

--- a/solution.py
+++ b/solution.py
@@ -152,7 +152,12 @@
             keep = jnp.where(upper_side, upper_part, lower_part)
             send = jnp.where(upper_side, lower_part, upper_part)
             owned = keep + partner(send, "slab", level)
-    gathered = lax.all_gather(owned[None], ("slab", "cross"), axis=0, tiled=True)
+    gathered = jnp.concatenate(
+        lax.all_to_all(
+            jnp.stack([owned[None]] * lax.axis_size(("slab", "cross"))), ("slab", "cross"), 0, 0
+        ),
+        axis=0,
+    )
     if fine_per_coarse <= planes:
         gathered = gathered.reshape(
             slab_count, cross_count, planes // fine_per_coarse, column_count

time: 173 us -> 137 us (0.79)
  waiting for transfers between devices: 59.6 us -> 28.4 us
  between operations: 14.3 us -> 0.94 us
  starting transfers between devices: 12.7 us -> 20.8 us
    all_gather x1 -> x0, waiting for transfers between devices: 54.9 us -> none  [body(): lax.all_gather(owned[None], ('slab', 'cross'), axis=0, tiled=True)]
    all_to_all x0 -> x1, waiting for transfers between devices: none -> 23.6 us  [body(): lax.all_to_all(jnp.stack([owned[None]] * lax.axis_size(('slab', 'cross'))...]
    all_to_all x0 -> x1, starting transfers between devices: none -> 8.32 us  [body(): lax.all_to_all(jnp.stack([owned[None]] * lax.axis_size(('slab', 'cross'))...]
    all_gather x1 -> x0, other arithmetic: 3.8 us -> none  [body(): lax.all_gather(owned[None], ('slab', 'cross'), axis=0, tiled=True)]
    all_to_all x0 -> x1, other arithmetic: none -> 2.57 us  [body(): lax.all_to_all(jnp.stack([owned[None]] * lax.axis_size(('slab', 'cross'))...]
    another operation x0 -> x1, local copies, waits for them, and re-layouts: none -> 1.92 us  [body(): jnp.stack([owned[None]] * lax.axis_size(('slab', 'cross')))]
  transfers between devices with their start and end apart: 5 -> 5, of which waited for: 3 -> 3; matrix products, arithmetic and copies ran while one was open for 11% -> 14% of each run, Pallas kernels for 0% -> 0%
where the time goes in v1:
time: 137 us; the launch traced here: 136 us
  local copies, waits for them, and re-layouts  44.3 us (32%)
  other arithmetic  41.7 us (30%)
  waiting for transfers between devices  28.4 us (21%)
  starting transfers between devices  20.8 us (15%)
    scatter-add x1, other arithmetic, body(): extended = jnp.zeros((fields, (planes + 2) * cross_cells), jnp.float32).a...  27 us
    all_to_all x1, waiting for transfers between devices, body(): lax.all_to_all(jnp.stack([owned[None]] * lax.axis_size(('slab', 'cross'))...  23.6 us
    gather x2, local copies, waits for them, and re-layouts, body(): ambient_layer_fields = jnp.take(gas_flat, fine_cell, axis=1)  15.3 us
    unnamed x19, local copies, waits for them, and re-layouts  9.02 us
    all_to_all x1, starting transfers between devices, body(): lax.all_to_all(jnp.stack([owned[None]] * lax.axis_size(('slab', 'cross'))...  8.32 us
    slice x1, local copies, waits for them, and re-layouts, body(): fine_source = extended[:, 1:planes + 1]  7.31 us
    ppermute x2, starting transfers between devices, shifted(): return lax.ppermute(shard, axis, pairs)  6.27 us
    div x4, other arithmetic, relax(): solution = (neighbours(solution) + coarse_source) / 6.0  5.57 us
  transfers between devices with their start and end apart: 5, of which 3 were waited for; matrix products, arithmetic and copies ran while one was open for 14% of the time, Pallas kernels for 0%

profile of v1, /device:TPU:0, one launch (start us, length us, event | category | flops | bytes accessed | tf_op | source)
XLA Modules:
  0.0 136.1 jit_solution(6537845980183800069)
XLA Ops:
  0.6 1.8 %fusion.50 = (f32[16,1,2048]{2,1,0:T(1,128)S(1)}, f32[16,1,2048]{2,1,0:T(1,128)S(1)}) fusion(f32[16,8,2048]{2,1,0:T(8,128)} %param.10), kind=kLoop, calls=%fused_computation.92 | loop fusion | bytes 524288 | tf_op jit(solution)/shard_map/slice | solution.py:22
  2.5 4.9 %collective-permute-start = (f32[16,1,2048]{2,0,1:T(8,128)S(1)}, f32[16,1,2048]{2,0,1:T(8,128)S(1)}, u32[]{:S(2)}, u32[]{:S(2)}) collective-permute-start(f32[16,1,2048]{2,0,1:T(8,128)S(1)} %copy.117), channel_id=1, source_target_pairs={{0,4},{4,8},{8,12},{12,16},{16,20},{20,24},{24,28},{1,5},{5,9},{9,... | collective-permute-start | bytes 393224 | tf_op jit(solution)/shard_map/ppermute | solution.py:24
  7.4 1.3 collective-permute-start.1
  8.7 0.7 compare_select_fusion
  9.5 0.7 compare_and_fusion
  10.2 0.7 select_bitcast_fusion.1
  10.9 0.1 copy.105
  11.1 3.2 %collective-permute-done.1 = f32[16,1,2048]{2,0,1:T(8,128)S(1)} collective-permute-done((f32[16,1,2048]{2,0,1:T(8,128)S(1)}, f32[16,1,2048]{2,0,1:T(8,128)S(1)}, u32[]{:S(2)}, u32[]{:S(2)}) %collective-permute-start.1) | collective-permute-done | bytes 131104 | tf_op jit(solution)/shard_map/ppermute | solution.py:25
  14.3 0.1 copy.106
  14.5 0.4 pad_maximum_fusion
  14.8 5.4 %copy.107 = f32[16,10,2048]{0,2,1:T(8,128)} copy(f32[16,10,2048]{2,1,0:T(8,128)S(1)} %pad_maximum_fusion) | data formatting | bytes 2621440 | tf_op jit(solution)/shard_map/concatenate | solution.py:26
  20.2 14.8 %gather_fusion = f32[4096,16]{1,0:T(8,128)S(1)} fusion(f32[16,20480]{0,1:T(8,128)} %bitcast.43, s32[4096]{0:T(1024)S(1)} %get-tuple-element.61), kind=kCustom, calls=%fused_computation | custom fusion | bytes 540672 | tf_op jit(solution)/shard_map/jit(_take)/gather | solution.py:117
  35.1 0.6 copy.108
  35.8 0.2 broadcast_add_fusion
  36.0 0.1 fusion.47
  36.1 0.2 multiply_subtract_fusion
  36.3 0.1 multiply_add_fusion
  36.4 0.1 fusion.33
  36.5 0.6 copy.109
  37.1 27.0 %scatter_custom_fusion = f32[16,20480]{0,1:T(8,128)} fusion(s32[4096]{0:T(1024)S(1)} %get-tuple-element.60, f32[4096,16]{1,0:T(8,128)S(1)} %copy.109, f32[]{:T(128)} %constant.122.clone.1), kind=kCustom, calls=%fused_computation.2 | custom fusion | flops 65536 | bytes 1310724 | tf_op jit(solution)/shard_map/scatter-add | solution.py:126
  64.0 2.1 %fusion.49 = (f32[16,1,2048]{0,2,1:T(8,128)S(1)}, f32[16,1,2048]{0,2,1:T(8,128)S(1)}, f32[16,1,2048]{0,2,1:T(8,128)S(1)}) fusion(f32[16,10,2048]{0,2,1:T(8,128)} %bitcast.37), kind=kLoop, calls=%fused_computation.91 | loop fusion | bytes 786432 | tf_op jit(solution)/shard_map/slice | solution.py:130
  66.1 1.0 copy.121
  67.1 1.3 collective-permute-start.2
  68.3 7.3 %slice.196 = f32[16,8,2048]{0,2,1:T(8,128)} slice(f32[16,10,2048]{0,2,1:T(8,128)} %bitcast.38), slice={[0:16], [1:9], [0:2048]} | slice | bytes 2097152 | tf_op jit(solution)/shard_map/slice | solution.py:131
  75.7 5.1 %copy.119 = f32[16,8,2048]{2,0,1:T(8,128)S(1)} copy(f32[16,8,2048]{0,2,1:T(8,128)} %slice.196) | data formatting | bytes 2097152
  80.8 0.3 copy.120
  81.1 0.3 copy.122
  81.4 5.0 %collective-permute-start.3 = (f32[16,2048]{1,0:T(8,128)S(1)}, f32[16,2048]{1,0:T(8,128)S(1)}, u32[]{:S(2)}, u32[]{:S(2)}) collective-permute-start(f32[16,2048]{1,0:T(8,128)S(1)} %bitcast.48), channel_id=1, source_target_pairs={{0,4},{4,8},{8,12},{12,16},{16,20},{20,24},{24,28},{1,5},{5,9},{9,... | collective-permute-start | bytes 393224 | tf_op jit(solution)/shard_map/ppermute | solution.py:33
  86.4 0.9 fusion.35
  87.3 1.6 %collective-permute-done.3 = f32[16,2048]{1,0:T(8,128)S(1)} collective-permute-done((f32[16,2048]{1,0:T(8,128)S(1)}, f32[16,2048]{1,0:T(8,128)S(1)}, u32[]{:S(2)}, u32[]{:S(2)}) %collective-permute-start.3) | collective-permute-done | bytes 131104 | tf_op jit(solution)/shard_map/ppermute | solution.py:33
  88.9 0.2 slice_reduce_fusion
  89.2 0.3 copy.114
  89.5 1.3 reduce_sum.42
  90.8 0.2 copy.115
  91.0 1.9 %stack.3 = f32[32,1,8192]{2,1,0:T(1,128)} broadcast(f32[8192]{0:T(1024)S(1)} %bitcast.50), dimensions={2} | broadcast | bytes 1081344 | tf_op jit(solution)/shard_map/stack | solution.py:157
  92.9 8.3 %all-to-all-start = ((f32[32,1,8192]{2,1,0:T(1,128)}), f32[32,1,8192]{2,1,0:T(1,128)S(1)}, u32[]{:S(2)}, u32[]{:S(2)}) async-start(f32[32,1,8192]{2,1,0:T(1,128)} %stack.3), calls=%async_computation | async-start | bytes 2097152 | tf_op jit(solution)/shard_map/all_to_all | solution.py:156
  101.3 0.1 fusion.42
  101.3 0.1 divide_add_fusion
  101.4 0.7 maximum_select_fusion
  102.1 1.6 %copy.116 = f32[16,8,2048]{2,1,0:T(8,128)} copy(f32[16,8,2048]{2,0,1:T(8,128)S(1)} %fusion.34) | data formatting | bytes 2097152
  103.7 23.6 %all-to-all-done = f32[32,1,8192]{2,1,0:T(1,128)S(1)} async-done(((f32[32,1,8192]{2,1,0:T(1,128)}), f32[32,1,8192]{2,1,0:T(1,128)S(1)}, u32[]{:S(2)}, u32[]{:S(2)}) %all-to-all-start) | async-done | bytes 1048608 | tf_op jit(solution)/shard_map/all_to_all | solution.py:156
  127.3 2.6 %reduce.5 = f32[32,8192]{1,0:T(8,128)S(1)} reduce(f32[32,1,8192]{2,1,0:T(1,128)S(1)} %all-to-all-done, f32[]{:T(128)} %constant.162), dimensions={1}, to_apply=%all_to_all.3.reduce_sub_computation | reduce | bytes 2097156 | tf_op jit(solution)/shard_map/all_to_all | solution.py:156
  129.8 0.6 copy.124
  130.5 0.1 broadcast_in_dim.29
  130.5 1.1 fusion.28
  131.7 1.1 fusion.8
  132.8 1.1 fusion.15
  134.0 2.1 %fusion.22 = f32[64,4096]{1,0:T(8,128)} fusion(f32[64,4096]{1,0:T(8,128)S(1)} %bitcast.42, f32[64,4096]{1,0:T(8,128)S(1)} %fusion.15, f32[4096]{0:T(1024)S(1)} %get-tuple-element.63, f32[4096]{0:T(1024)S(1)} %get-tuple-element.62), kind=kLoop, calls=%fused_computation.37 | loop fusion | flops 2359296 | bytes 3178496 | tf_op jit(solution)/shard_map/div | solution.py:104
  (21 shorter events, 0.3 us)
Async XLA Ops:
  0.6 13.8 %copy-start = (f32[16,8,2048]{2,1,0:T(8,128)S(1)}, f32[16,8,2048]{2,1,0:T(8,128)}, u32[]{:S(2)}) copy-start(f32[16,8,2048]{2,1,0:T(8,128)} %param.10) | copy-start | bytes 3145732
  2.5 8.4 %collective-permute-start = (f32[16,1,2048]{2,0,1:T(8,128)S(1)}, f32[16,1,2048]{2,0,1:T(8,128)S(1)}, u32[]{:S(2)}, u32[]{:S(2)}) collective-permute-start(f32[16,1,2048]{2,0,1:T(8,128)S(1)} %copy.117), channel_id=1, source_target_pairs={{0,4},{4,8},{8,12},{12,16},{16,20},{20,24},{24,28},{1,5},{5,9},{9,... | collective-permute-start | bytes 393224 | tf_op jit(solution)/shard_map/ppermute | solution.py:24
  7.4 6.9 %collective-permute-start.1 = (f32[16,1,2048]{2,0,1:T(8,128)S(1)}, f32[16,1,2048]{2,0,1:T(8,128)S(1)}, u32[]{:S(2)}, u32[]{:S(2)}) collective-permute-start(f32[16,1,2048]{2,0,1:T(8,128)S(1)} %copy.118), channel_id=1, source_target_pairs={{4,0},{8,4},{12,8},{16,12},{20,16},{24,20},{28,24},{5,1},{9,5},{13... | collective-permute-start | bytes 393224 | tf_op jit(solution)/shard_map/ppermute | solution.py:25
  20.2 15.4 %copy-start.1 = (f32[5,4096]{1,0:T(8,128)S(1)}, f32[5,4096]{1,0:T(8,128)}, u32[]{:S(2)}) copy-start(f32[5,4096]{1,0:T(8,128)} %param.11) | copy-start | bytes 245764
  35.0 1.0 copy-start.2
  35.0 0.9 copy-start.4
  67.1 19.3 %collective-permute-start.2 = (f32[16,2048]{1,0:T(8,128)}, f32[16,2048]{1,0:T(8,128)}, u32[]{:S(2)}, u32[]{:S(2)}) collective-permute-start(f32[16,2048]{1,0:T(8,128)} %bitcast.13), channel_id=1, source_target_pairs={{4,0},{8,4},{12,8},{16,12},{20,16},{24,20},{28,24},{5,1},{9,5},{13... | collective-permute-start | bytes 393224 | tf_op jit(solution)/shard_map/ppermute | solution.py:33
  81.4 7.5 %collective-permute-start.3 = (f32[16,2048]{1,0:T(8,128)S(1)}, f32[16,2048]{1,0:T(8,128)S(1)}, u32[]{:S(2)}, u32[]{:S(2)}) collective-permute-start(f32[16,2048]{1,0:T(8,128)S(1)} %bitcast.48), channel_id=1, source_target_pairs={{0,4},{4,8},{8,12},{12,16},{16,20},{20,24},{24,28},{1,5},{5,9},{9,... | collective-permute-start | bytes 393224 | tf_op jit(solution)/shard_map/ppermute | solution.py:33
  90.8 10.5 %copy-start.3 = (s32[32]{0:T(128)S(1)}, s32[32]{0:T(128)}, u32[]{:S(2)}) copy-start(s32[32]{0:T(128)} %param.15) | copy-start | bytes 388
  92.9 34.4 %all-to-all-start = ((f32[32,1,8192]{2,1,0:T(1,128)}), f32[32,1,8192]{2,1,0:T(1,128)S(1)}, u32[]{:S(2)}, u32[]{:S(2)}) async-start(f32[32,1,8192]{2,1,0:T(1,128)} %stack.3), calls=%async_computation | async-start | bytes 2097152 | tf_op jit(solution)/shard_map/all_to_all | solution.py:156
